TPU v7x, 128 devices: a whole 4x4x4 slice. The times are simulated.
128 devices in a mesh: blk: 16 (over z_lo, y, core), seq: 8 (over x, z_hi).
Axes of the slice: x: 4, y: 4, z: 4 (z_hi: 2, z_lo: 2; z = z_hi * 2 + z_lo), core: 2. Of those that a mesh axis runs over, the one named last changes fastest.
Arguments:
- layer_input: bfloat16 [16, 1024, 8192], P('blk', 'seq'), may hold values from -6 to 6
- queries: bfloat16 [16, 1024, 4096], P('blk', 'seq'), may hold values from -48 to 48, as said below
- grad_out: bfloat16 [16, 1024, 4096], P('blk', 'seq'), may hold values from -6 to 6
- segment_ids: int32 [16, 1024], P('blk', 'seq'), may hold values from 0 to 3, never falling along the last dimension, each value on 1 to 512 neighbouring positions
- kv_weight: bfloat16 [8192, 1024], P(('blk', 'seq')), may hold values from -0.0625 to 0.0625
- norm_gain: float32 [8192], replicated, may hold values from 0.5 to 1.5
Outputs:
- attended: bfloat16 [16, 1024, 4096], P('blk', 'seq')
- grad_queries: bfloat16 [16, 1024, 4096], P('blk', 'seq')
- grad_input: bfloat16 [16, 1024, 8192], P('blk', 'seq')
- grad_weight: float32 [8192, 1024], P(('blk', 'seq'))
- grad_gain: float32 [8192], replicated
Inputs may be any that keep to these rules, and one draw needn't show every extreme that they name: Projected queries; some rows may be larger than others.
All inputs are finite; a program needn't handle non-finite values.
Results may differ from a plain program's by a relative error of at most 0.02.
The roundings to bfloat16 on the way count: a program that leaves them out, or rounds other values in their place, can miss the bound.
Values may be sent and summed in bfloat16 or wider, within the bound.
No kernel may reach another device: no remote copies, remote signals or barrier semaphores. Data moves between devices by JAX's collectives and lax.ppermute only.
A program may use at most 128 MiB of HBM per device.

v0:
```python
import jax
import jax.numpy as jnp
from jax import lax
from jax.sharding import PartitionSpec as P

HEAD = 128
epsilon = 1e-05


def cut_along(shard, dim, length):
    lengths = shard.shape
    pieces = shard.reshape(*lengths[:dim], length, lengths[dim] // length, *lengths[dim + 1 :])
    return jnp.moveaxis(pieces, dim, 0)


def sum_at_owner(shard, axis, dim):
    length = lax.axis_size(axis)
    pieces = lax.all_to_all(cut_along(shard, dim, length), axis, 0, 0, tiled=True)
    return jnp.sum(pieces, axis=0)


def shards(layer_input, queries, grad_out, segment_ids, kv_weight, norm_gain):
    f32 = jnp.float32
    tok_rows = layer_input.shape[1]
    model_width = layer_input.shape[2]
    seq_devices = lax.axis_size("seq")
    blk_devices = lax.axis_size("blk")
    length = tok_rows * seq_devices
    seq_index = lax.axis_index("seq")
    kv_total = kv_weight.shape[1]
    kv_width = kv_total // 2
    kv_heads = kv_width // HEAD
    query_count = queries.shape[2] // HEAD
    group_size = query_count // kv_heads
    score_scale = HEAD ** (-0.5)
    piece_cols = kv_weight.shape[0]
    source = layer_input[0].astype(f32)
    inv_rms = lax.rsqrt(jnp.mean(source * source, axis=1, keepdims=True) + epsilon)
    scaled = source * inv_rms
    normed = (scaled * norm_gain).astype(jnp.bfloat16)
    split_cols = normed.reshape(tok_rows, blk_devices, seq_devices, piece_cols)
    columns = lax.all_to_all(split_cols, "seq", split_axis=2, concat_axis=0, tiled=True).reshape(
        length, blk_devices * piece_cols
    )
    weight_slab = lax.all_gather(kv_weight, "blk", axis=0, tiled=True)
    query_heads = queries[0].reshape(tok_rows, kv_heads, group_size, HEAD)
    query_pos = seq_index * tok_rows + jnp.arange(tok_rows, dtype=jnp.int32)
    query_doc = segment_ids[0]
    grad_heads = grad_out[0].reshape(tok_rows, kv_heads, group_size, HEAD).transpose(1, 2, 0, 3)

    def scores_of(kv_piece, doc_piece):
        rows_here = kv_piece.shape[0]
        key_heads = kv_piece[:, :kv_width].reshape(rows_here, kv_heads, HEAD)
        raw_scores = (
            jnp.einsum("qgjd,kgd->gjqk", query_heads, key_heads, preferred_element_type=f32)
            * score_scale
        )
        key_pos = jnp.arange(rows_here, dtype=jnp.int32)
        allowed = (key_pos[None, :] <= query_pos[:, None]) & (
            doc_piece[None, :] == query_doc[:, None]
        )
        return (jnp.where(allowed, raw_scores, -1e30), allowed, key_heads)

    stat_shape = (kv_heads, group_size, tok_rows, 1)
    kv_own = sum_at_owner(
        jnp.dot(columns, weight_slab, preferred_element_type=f32), "seq", 0
    ).astype(jnp.bfloat16)
    row_max = jnp.full(stat_shape, -1e30, f32)
    kv_piece = lax.all_gather(kv_own, "seq", axis=0, tiled=True)
    doc_piece = lax.all_gather(query_doc, "seq", axis=0, tiled=True)
    rows_here = kv_piece.shape[0]
    masked, allowed, key_heads = scores_of(kv_piece, doc_piece)
    new_max = jnp.maximum(row_max, jnp.max(masked, axis=-1, keepdims=True))
    expo_terms = jnp.where(allowed, jnp.exp(masked - new_max), 0.0)
    value_heads = kv_piece[:, kv_width:].reshape(rows_here, kv_heads, HEAD)
    weights = expo_terms.astype(jnp.bfloat16)
    weighted = jnp.einsum("gjqk,kgd->gjqd", weights, value_heads, preferred_element_type=f32)
    row_sum = jnp.sum(expo_terms, axis=-1, keepdims=True)
    row_max, row_sum, weighted = (new_max, row_sum, weighted)
    summed = weighted / row_sum
    attended = (
        summed.transpose(2, 0, 1, 3).reshape(tok_rows, query_count * HEAD).astype(jnp.bfloat16)
    )
    log_total = row_max + jnp.log(row_sum)
    attended_heads = attended.reshape(tok_rows, kv_heads, group_size, HEAD).transpose(1, 2, 0, 3)
    row_delta = jnp.sum(grad_heads.astype(f32) * attended_heads.astype(f32), axis=-1, keepdims=True)
    kv_piece = lax.all_gather(kv_own, "seq", axis=0, tiled=True)
    doc_piece = lax.all_gather(query_doc, "seq", axis=0, tiled=True)
    rows_here = kv_piece.shape[0]
    masked, allowed, key_heads = scores_of(kv_piece, doc_piece)
    softmax_probs = jnp.where(allowed, jnp.exp(masked - log_total), 0.0)
    value_heads = kv_piece[:, kv_width:].reshape(rows_here, kv_heads, HEAD)
    grad_probs = jnp.einsum("gjqd,kgd->gjqk", grad_heads, value_heads, preferred_element_type=f32)
    grad_scores = (softmax_probs * (grad_probs - row_delta)).astype(jnp.bfloat16)
    probs_half = softmax_probs.astype(jnp.bfloat16)
    grad_values = jnp.einsum("gjqk,gjqd->kgd", probs_half, grad_heads, preferred_element_type=f32)
    grad_keys = (
        jnp.einsum("gjqk,qgjd->kgd", grad_scores, query_heads, preferred_element_type=f32)
        * score_scale
    )
    grad_query = (
        jnp.einsum("gjqk,kgd->qgjd", grad_scores, key_heads, preferred_element_type=f32)
        * score_scale
    )
    new_rows = jnp.concatenate(
        [grad_keys.reshape(rows_here, kv_width), grad_values.reshape(rows_here, kv_width)], axis=1
    )
    grad_rows = new_rows
    grad_query, grad_rows = (grad_query, grad_rows)
    grad_own = sum_at_owner(grad_rows, "seq", 0).astype(jnp.bfloat16)
    grad_kv = lax.all_gather(grad_own, "seq", axis=0, tiled=True)
    grad_queries = grad_query.reshape(tok_rows, query_count * HEAD).astype(jnp.bfloat16)
    slab_back = lax.all_gather(kv_weight, "blk", axis=0, tiled=True)
    grad_weight = lax.psum_scatter(
        lax.dot_general(columns, grad_kv, (((0,), (0,)), ((), ())), preferred_element_type=f32),
        "blk",
        scatter_dimension=0,
        tiled=True,
    )
    grad_cols = lax.dot_general(
        grad_kv, slab_back, (((1,), (1,)), ((), ())), preferred_element_type=f32
    ).astype(jnp.bfloat16)
    grad_cols = grad_cols.reshape(length, blk_devices, 1, piece_cols)
    grad_normed = lax.all_to_all(grad_cols, "seq", split_axis=0, concat_axis=2, tiled=True).reshape(
        tok_rows, model_width
    )
    grad_norm = grad_normed.astype(f32)
    grad_gain = lax.psum(jnp.sum(grad_norm * scaled, axis=0), ("blk", "seq"))
    grad_hat = grad_norm * norm_gain
    grad_input = inv_rms * (grad_hat - scaled * jnp.mean(grad_hat * scaled, axis=1, keepdims=True))
    return (
        attended[None],
        grad_queries[None],
        grad_input.astype(jnp.bfloat16)[None],
        grad_weight,
        grad_gain,
    )


def solution(mesh):
    in_specs = (
        P("blk", "seq", None),
        P("blk", "seq", None),
        P("blk", "seq", None),
        P("blk", "seq"),
        P(("blk", "seq"), None),
        P(),
    )
    out_specs = (
        P("blk", "seq", None),
        P("blk", "seq", None),
        P("blk", "seq", None),
        P(("blk", "seq"), None),
        P(),
    )
    return jax.shard_map(shards, mesh=mesh, in_specs=in_specs, out_specs=out_specs, check_vma=False)
```

profile of v0, /device:TPU:1, one launch (start us, length us, event | category | flops | bytes accessed | tf_op | source)
XLA Modules:
  0.0 534.6 jit_solution(473694179402004484)
XLA Ops:
  7.2 0.0 all-gather.5.cloned.1.call-start
  7.2 0.7 all-gather.5.cloned.1.call-update
  7.9 0.0 all-gather.7.cloned.1.call-start
  8.0 3.2 copy.148
  11.2 2.2 convert_element_type.140
  13.4 0.1 mul.121
  13.5 1.1 multiply_reduce_fusion.2
  14.6 2.9 multiply_convert_fusion
  17.5 0.2 copy.149
  17.7 38.3 %all_to_all.34 = bf16[128,16,8,64]{0,3,1,2:T(8,128)(2,1)} all-to-all(bf16[128,16,8,64]{0,3,1,2:T(8,128)(2,1)S(1)} %copy.149), channel_id=1, replica_groups=mesh['blk'=16,'seq'=8] {'seq'}, dimensions={2} | all-to-all | bytes 4194304 | tf_op jit(solution)/shard_map/all_to_all | solution.py:42
  56.0 8.3 %all-gather.5.cloned.1.call-done = bf16[1024,1024]{1,0:T(8,128)(2,1)} async-done(((bf16[64,1024]{1,0:T(8,128)(2,1)}), bf16[1024,1024]{1,0:T(8,128)(2,1)}) %all-gather.5.cloned.1.call-update) | async-done | bytes 2097168 | tf_op jit(solution)/shard_map/all_gather | solution.py:45
  64.3 4.6 fusion.22
  68.9 55.1 %all_to_all.35 = f32[8,128,1024]{2,1,0:T(8,128)} all-to-all(f32[8,128,1024]{2,1,0:T(8,128)S(1)} %fusion.22), channel_id=1, replica_groups=mesh['blk'=16,'seq'=8] {'seq'}, dimensions={0} | all-to-all | bytes 8388608 | tf_op jit(solution)/shard_map/all_to_all | solution.py:18
  124.1 3.4 reduce_sum.66
  127.5 0.0 all-gather.9.cloned.1.call-start
  127.6 1.2 copy.192
  128.8 2.3 copy.156
  131.0 17.1 %all-gather = s32[1,1024]{1,0:T(1,128)S(1)} all-gather(s32[1,128]{1,0:T(1,128)S(1)} %copy-done.8), channel_id=2, replica_groups=mesh['blk'=16,'seq'=8] {'seq'}, dimensions={1}, use_global_device_ids=true | all-gather | bytes 4608 | tf_op jit(solution)/shard_map/all_gather | solution.py:70
  148.2 0.2 fusion.29
  148.4 30.2 %all-gather.7.cloned.1.call-done = bf16[1024,1024]{1,0:T(8,128)(2,1)} async-done(((bf16[128,1024]{1,0:T(8,128)(2,1)}), bf16[1024,1024]{1,0:T(8,128)(2,1)}) %all-gather.7.cloned.1.call-update) | async-done | bytes 2097168 | tf_op jit(solution)/shard_map/all_gather | solution.py:69
  178.5 3.0 fusion.32
  181.5 1.5 copy.151
  183.0 9.1 %fusion.33 = (f32[4,8,128]{2,1,0:T(8,128)S(1)}, f32[4,8,128,1024]{2,3,1,0:T(8,128)}) fusion(bf16[1024,4,128,1]{0,2,3,1:T(8,128)(2,1)S(1)} %bitcast.122, bf16[128,4,8,128]{3,2,1,0:T(8,128)(2,1)} %bitcast.124, pred[128,1024]{0,1:T(8,128)(4,1)S(1)} %fusion.29), kind=kOutput, calls=%fused_computation.52 | convolution fusion | flops 1086320640 | bytes 19021824 | tf_op jit(solution)/shard_map/qgjd,kgd->gjqk/dot_general | solution.py:55
  192.1 2.3 copy.154
  194.4 8.7 %fusion.1 = f32[4,8,128]{2,1,0:T(8,128)S(1)} fusion(f32[4,8,128,1024]{2,3,1,0:T(8,128)} %get-tuple-element.45, f32[4,8,128]{2,1,0:T(8,128)S(1)} %broadcast_maximum_fusion, pred[128,1024]{0,1:T(8,128)(4,1)S(1)} %fusion.29), kind=kLoop, calls=%fused_computation.5 | loop fusion | flops 12578816 | bytes 16941056 | tf_op jit(solution)/shard_map/reduce_sum | solution.py:78
  203.1 9.9 %fusion.21 = (bf16[128,4,8,128]{0,3,2,1:T(8,128)(2,1)}, f32[4,8,128,128]{2,3,1,0:T(8,128)S(1)}) fusion(f32[128,4,8]{0,2,1:T(8,128)S(1)} %bitcast.140, bf16[1024,4,128,1]{0,2,3,1:T(8,128)(2,1)S(1)} %bitcast.138, f32[4,8,128,1024]{2,3,1,0:T(8,128)} %get-tuple-element.45, f32[4,8,128]{2,1,0:T(8,128)S(1)} %broadcast_maximum_fusion, ...), kind=kOutput, calls=%fused_computation.32 | convolution fusion | flops 1087373312 | bytes 21135360 | tf_op jit(solution)/shard_map/gjqk,kgd->gjqd/dot_general | solution.py:77
  212.9 0.5 multiply_reduce_fusion.3
  213.4 9.5 %fusion.24 = f32[1024,4,128]{2,0,1:T(8,128)} fusion(bf16[4,8,128,128]{2,3,1,0:T(8,128)(2,1)S(1)} %bitcast.131, f32[4,8,128,1024]{2,3,1,0:T(8,128)} %get-tuple-element.45, f32[4,8,128]{2,1,0:T(8,128)S(1)} %log_add_fusion, pred[128,1024]{0,1:T(8,128)(4,1)S(1)} %fusion.29), kind=kOutput, calls=%fused_computation.39 | convolution fusion | flops 1086324736 | bytes 20070400 | tf_op jit(solution)/shard_map/gjqk,gjqd->kgd/dot_general | solution.py:96
  222.9 10.9 %fusion = bf16[4,8,128,1024]{2,3,1,0:T(8,128)(2,1)} fusion(f32[4,8,128,1024]{2,3,1,0:T(8,128)} %get-tuple-element.45, bf16[1024,4,128,1]{0,2,3,1:T(8,128)(2,1)S(1)} %bitcast.139, bf16[4,8,128,128]{2,3,1,0:T(8,128)(2,1)S(1)} %bitcast.132, f32[4,8,128]{2,1,0:T(8,128)S(1)} %multiply_reduce_fusion.3, f32[4,8,128]{2,1,0:T(8,128)S(1)} %log_add_fusion, ...), kind=kOutput, calls=%fused_computation.1 | convolution fusion | flops 1094713344 | bytes 27426816 | tf_op jit(solution)/shard_map/gjqd,kgd->gjqk/dot_general | solution.py:93
  233.8 2.9 copy.163
  236.7 3.5 copy.194
  240.2 7.1 %fusion.20 = f32[1024,4,128]{2,0,1:T(8,128)} fusion(bf16[4,8,128,1024]{2,3,1,0:T(8,128)(2,1)} %fusion, bf16[128,4,8,128]{3,2,1,0:T(8,128)(2,1)S(1)} %bitcast.125), kind=kOutput, calls=%fused_computation.30 | convolution fusion | flops 1074266112 | bytes 11534336 | tf_op jit(solution)/shard_map/gjqk,qgjd->kgd/dot_general | solution.py:98
  247.3 2.9 copy.161
  250.2 2.2 copy.193
  252.4 0.3 pad_maximum_fusion
  252.7 0.8 copy.164
  253.5 50.9 %all_to_all.36 = f32[8,128,1024]{1,2,0:T(8,128)} all-to-all(f32[8,128,1024]{1,2,0:T(8,128)S(1)} %copy.164), channel_id=1, replica_groups=mesh['blk'=16,'seq'=8] {'seq'}, dimensions={0} | all-to-all | bytes 8388608 | tf_op jit(solution)/shard_map/all_to_all | solution.py:18
  304.4 3.2 reduce_sum.69
  307.6 0.2 reduce-scatter.2.cloned.1.call-start
  307.8 4.7 copy.171
  312.5 51.4 %all-gather.9.cloned.1.call-done = bf16[1024,1024]{0,1:T(8,128)(2,1)} async-done(((bf16[128,1024]{0,1:T(8,128)(2,1)}), bf16[1024,1024]{0,1:T(8,128)(2,1)}) %all-gather.9.cloned.1.call-update) | async-done | bytes 2097168 | tf_op jit(solution)/shard_map/all_gather | solution.py:111
  363.9 6.5 %fusion.17 = f32[1024,1024]{1,0:T(8,128)} fusion(bf16[1024,1024]{0,1:T(8,128)(2,1)} %all-gather.9.cloned.1.call-done, bf16[128,8,8,128]{3,2,1,0:T(8,128)(2,1)} %bitcast.135), kind=kOutput, calls=%fused_computation.26 | convolution fusion | flops 2147483648 | bytes 8388608 | tf_op jit(solution)/shard_map/dot_general | solution.py:115
  370.4 5.9 %convolution_convert_fusion = bf16[1024,1024]{0,1:T(8,128)(2,1)} fusion(bf16[1024,1024]{1,0:T(8,128)(2,1)} %all-gather.5.cloned.1.call-done, bf16[1024,1024]{0,1:T(8,128)(2,1)} %all-gather.9.cloned.1.call-done), kind=kOutput, calls=%fused_computation.38 | convolution fusion | flops 2148532224 | bytes 6291456 | tf_op jit(solution)/shard_map/dot_general | solution.py:120
  376.3 6.2 %copy.166 = bf16[1024,16,1,64]{3,1,2,0:T(8,128)(2,1)} copy(bf16[1024,16,1,64]{0,3,1,2:T(8,128)(2,1)} %bitcast.134) | data formatting | bytes 4194304 | tf_op jit(solution)/shard_map/reshape | solution.py:123
  382.5 7.6 %reshape.223 = bf16[8,2,65536]{2,1,0:T(2,128)(2,1)} reshape(bf16[1024,1,16,64]{3,2,1,0:T(8,128)(2,1)} %bitcast.119) | data formatting | bytes 4194304
  390.1 4.6 all-to-all-start.3
  394.6 1.0 copy.169
  395.7 2.3 copy.173
  397.9 5.6 %multiply_convert_fusion.1 = bf16[4,128,8,128]{3,1,2,0:T(8,128)(2,1)} fusion(bf16[1024,4,128,1]{0,2,3,1:T(8,128)(2,1)S(1)} %bitcast.123, bf16[4,8,128,1024]{2,3,1,0:T(8,128)(2,1)} %fusion), kind=kOutput, calls=%fused_computation.35 | convolution fusion | flops 1074790400 | bytes 10485760 | tf_op jit(solution)/shard_map/gjqk,kgd->qgjd/dot_general | solution.py:102
  403.6 2.3 copy.174
  405.9 22.6 %all-to-all-done.3 = bf16[8,2,65536]{2,1,0:T(2,128)(2,1)} async-done(((bf16[8,2,65536]{2,1,0:T(2,128)(2,1)}), bf16[8,2,65536]{2,1,0:T(2,128)(2,1)}, u32[]{:S(2)}, u32[]{:S(2)}) %all-to-all-start.3) | async-done | bytes 2097184 | tf_op jit(solution)/shard_map/all_to_all | solution.py:124
  428.4 7.4 %reshape.224 = bf16[1024,1,16,64]{3,2,1,0:T(8,128)(2,1)} reshape(bf16[8,2,65536]{2,1,0:T(2,128)(2,1)} %all-to-all-done.3) | data formatting | bytes 4194304
  435.8 5.5 %copy.167 = bf16[1024,16,1,64]{0,3,2,1:T(8,128)(2,1)} copy(bf16[1024,16,1,64]{3,1,2,0:T(8,128)(2,1)} %bitcast.120) | data formatting | bytes 4194304 | tf_op jit(solution)/shard_map/all_to_all | solution.py:124
  441.3 2.1 convert_element_type.146
  443.4 1.0 copy.195
  444.4 0.7 copy.168
  445.2 1.4 copy-done
  446.6 0.1 copy-done.4
  446.7 4.8 multiply_reduce_fusion
  451.5 4.4 fusion.16
  455.9 4.1 copy.175
  460.0 0.2 copy.172
  460.2 0.1 reduce_sum.72
  460.2 67.6 %psum.7 = f32[8192]{0:T(1024)} all-reduce(f32[8192]{0:T(1024)S(1)} %reduce_sum.72), channel_id=1, replica_groups=mesh['blk'=16,'seq'=8] {'blk','seq'}, use_global_device_ids=true, to_apply=%region_9.10 | all-reduce | flops 8192 | bytes 65536 | tf_op jit(solution)/shard_map/psum | solution.py:128
  (25 shorter events, 0.1 us)
Async XLA Ops:
  7.2 57.1 %all-gather.5.cloned.1.call-start = ((), (), s32[]{:S(2)}) async-start(), calls=%async_computation.5 | async-start | bytes 2228224 | tf_op jit(solution)/shard_map/all_gather | solution.py:45
  7.9 5.5 %copy-start.7 = (f32[8192]{0:T(1024)S(1)}, f32[8192]{0:T(1024)}, u32[]{:S(2)}) copy-start(f32[8192]{0:T(1024)} %param.11) | copy-start | bytes 98308
  7.9 170.6 %all-gather.7.cloned.1.call-start = ((), (), s32[]{:S(2)}) async-start(), calls=%async_computation.6 | async-start | bytes 2359296 | tf_op jit(solution)/shard_map/all_gather | solution.py:69
  124.0 3.5 copy-start.5
  124.0 7.0 %copy-start.8 = (s32[1,128]{1,0:T(1,128)S(1)}, s32[1,128]{1,0:T(1,128)}, u32[]{:S(2)}) copy-start(s32[1,128]{1,0:T(1,128)} %param.9) | copy-start | bytes 1540
  127.5 236.4 %all-gather.9.cloned.1.call-start = ((), (), s32[]{:S(2)}) async-start(), calls=%async_computation.7 | async-start | bytes 2359296 | tf_op jit(solution)/shard_map/all_gather | solution.py:111
  194.4 8.7 %copy-start.6 = (bf16[1024,512]{0,1:T(8,128)(2,1)S(1)}, bf16[1024,512]{0,1:T(8,128)(2,1)}, u32[]{:S(2)}) copy-start(bf16[1024,512]{0,1:T(8,128)(2,1)} %copy.154) | copy-start | bytes 3145732
  203.1 9.9 %copy-start.3 = (bf16[1,128,4096]{1,2,0:T(8,128)(2,1)S(1)}, bf16[1,128,4096]{1,2,0:T(8,128)(2,1)}, u32[]{:S(2)}) copy-start(bf16[1,128,4096]{1,2,0:T(8,128)(2,1)} %copy.156) | copy-start | bytes 3145732
  236.7 3.5 copy-start.1
  250.2 2.2 copy-start.2
  307.6 220.3 %reduce-scatter.2.cloned.1.call-start = ((), (), s32[]{:S(2)}) async-start(), calls=%async_computation.8 | async-start | bytes 4456448 | tf_op jit(solution)/shard_map/reduce_scatter | solution.py:114
  390.1 38.4 %all-to-all-start.3 = ((bf16[8,2,65536]{2,1,0:T(2,128)(2,1)}), bf16[8,2,65536]{2,1,0:T(2,128)(2,1)}, u32[]{:S(2)}, u32[]{:S(2)}) async-start(bf16[8,2,65536]{2,1,0:T(2,128)(2,1)} %reshape.223), calls=%async_computation.3 | async-start | bytes 4194304 | tf_op jit(solution)/shard_map/all_to_all | solution.py:124
  444.4 2.2 copy-start
  444.4 2.3 copy-start.4
Sparse Core Ops, SparseCore 0:
  9.7 54.5 all-gather.4
  127.6 50.8 all-gather.6
  307.7 56.0 all-gather.8
  370.5 72.2 reduce-scatter.1
where the time goes:
time: 540 us; the launch traced here: 535 us
  blocking collectives  229 us (42%)
  waiting for transfers between devices  113 us (21%)
  local copies, waits for them, and re-layouts  70.6 us (13%)
  matrix products  69.1 us (13%)
  other arithmetic  33.7 us (6%)
  between operations  14.2 us (3%)
    all_to_all x2, blocking collectives, sum_at_owner(): lax.all_to_all(cut_along(shard, dim, length), axis, 0, 0, tiled=True)  106 us
    psum x1, blocking collectives, shards(): grad_gain = lax.psum(jnp.sum(grad_norm * scaled, axis=0), ('blk', 'seq'))  67.6 us
    all_gather x1, waiting for transfers between devices, shards(): grad_kv = lax.all_gather(grad_own, 'seq', axis=0, tiled=True)  51.4 us
    unnamed x29, local copies, waits for them, and re-layouts  38.6 us
    all_to_all x1, blocking collectives, shards(): lax.all_to_all(split_cols, 'seq', split_axis=2, concat_axis=0, tiled=True)  38.3 us
    all_gather x1, waiting for transfers between devices, shards(): kv_piece = lax.all_gather(kv_own, 'seq', axis=0, tiled=True)  30.2 us
    all_to_all x1, waiting for transfers between devices, shards(): lax.all_to_all(grad_cols, 'seq', split_axis=0, concat_axis=2, tiled=True)  22.6 us
    all_gather x1, blocking collectives, shards(): doc_piece = lax.all_gather(query_doc, 'seq', axis=0, tiled=True)  17.1 us
  transfers between devices with their start and end apart: 5, of which 4 were waited for; matrix products, arithmetic and copies ran while one was open for 15% of the time, Pallas kernels for 0%

commit v1 on v0

--- a/solution.py
+++ b/solution.py
@@ -121,9 +121,10 @@
         grad_kv, slab_back, (((1,), (1,)), ((), ())), preferred_element_type=f32
     ).astype(jnp.bfloat16)
     grad_cols = grad_cols.reshape(length, blk_devices, 1, piece_cols)
-    grad_normed = lax.all_to_all(grad_cols, "seq", split_axis=0, concat_axis=2, tiled=True).reshape(
-        tok_rows, model_width
-    )
+    grad_normed = jnp.concatenate(
+        lax.all_to_all(jnp.stack(jnp.split(grad_cols, lax.axis_size("seq"), axis=0)), "seq", 0, 0),
+        axis=2,
+    ).reshape(tok_rows, model_width)
     grad_norm = grad_normed.astype(f32)
     grad_gain = lax.psum(jnp.sum(grad_norm * scaled, axis=0), ("blk", "seq"))
     grad_hat = grad_norm * norm_gain

time: 540 us -> 506 us (0.937)
  local copies, waits for them, and re-layouts: 70.6 us -> 45.6 us
    unnamed x29, local copies, waits for them, and re-layouts: 38.6 us -> 26.1 us
    reshape x1 -> x0, local copies, waits for them, and re-layouts: 6.19 us -> none  [shards(): grad_cols = grad_cols.reshape(length, blk_devices, 1, piece_cols)]
    all_to_all x1 -> x0, local copies, waits for them, and re-layouts: 5.46 us -> none  [shards(): lax.all_to_all(grad_cols, 'seq', split_axis=0, concat_axis=2, tiled=True)]
  transfers between devices with their start and end apart: 5 -> 5, of which waited for: 4 -> 4; matrix products, arithmetic and copies ran while one was open for 15% -> 10% of each run, Pallas kernels for 0% -> 0%
where the time goes in v1:
time: 506 us; the launch traced here: 505 us
  blocking collectives  231 us (46%)
  waiting for transfers between devices  113 us (22%)
  matrix products  67.3 us (13%)
  local copies, waits for them, and re-layouts  45.6 us (9%)
  other arithmetic  30.1 us (6%)
  between operations  14 us (3%)
    all_to_all x2, blocking collectives, sum_at_owner(): lax.all_to_all(cut_along(shard, dim, length), axis, 0, 0, tiled=True)  106 us
    psum x1, blocking collectives, shards(): grad_gain = lax.psum(jnp.sum(grad_norm * scaled, axis=0), ('blk', 'seq'))  69.3 us
    all_gather x1, waiting for transfers between devices, shards(): grad_kv = lax.all_gather(grad_own, 'seq', axis=0, tiled=True)  51.5 us
    all_to_all x1, blocking collectives, shards(): lax.all_to_all(split_cols, 'seq', split_axis=2, concat_axis=0, tiled=True)  38.3 us
    all_gather x1, waiting for transfers between devices, shards(): kv_piece = lax.all_gather(kv_own, 'seq', axis=0, tiled=True)  30.3 us
    unnamed x29, local copies, waits for them, and re-layouts  26.1 us
    all_to_all x1, waiting for transfers between devices, shards(): lax.all_to_all(jnp.stack(jnp.split(grad_cols, lax.axis_size('seq'), axis=...  22 us
    all_gather x1, blocking collectives, shards(): doc_piece = lax.all_gather(query_doc, 'seq', axis=0, tiled=True)  17 us
  transfers between devices with their start and end apart: 5, of which 4 were waited for; matrix products, arithmetic and copies ran while one was open for 10% of the time, Pallas kernels for 0%

profile of v1, /device:TPU:1, one launch (start us, length us, event | category | flops | bytes accessed | tf_op | source)
XLA Modules:
  0.0 505.3 jit_solution(345591463853602846)
XLA Ops:
  7.2 0.0 all-gather.5.cloned.1.call-start
  7.2 0.7 all-gather.5.cloned.1.call-update
  7.9 0.0 all-gather.7.cloned.1.call-start
  7.9 3.2 copy.51
  11.2 2.2 convert_element_type.135
  13.4 0.1 mul.121
  13.5 1.1 multiply_reduce_fusion
  14.6 2.9 multiply_convert_fusion
  17.5 0.2 copy.52
  17.7 38.3 %all_to_all.30 = bf16[128,16,8,64]{0,3,1,2:T(8,128)(2,1)} all-to-all(bf16[128,16,8,64]{0,3,1,2:T(8,128)(2,1)S(1)} %copy.52), channel_id=1, replica_groups=mesh['blk'=16,'seq'=8] {'seq'}, dimensions={2} | all-to-all | bytes 4194304 | tf_op jit(solution)/shard_map/all_to_all | solution.py:42
  56.0 8.3 %all-gather.5.cloned.1.call-done = bf16[1024,1024]{1,0:T(8,128)(2,1)} async-done(((bf16[64,1024]{1,0:T(8,128)(2,1)}), bf16[1024,1024]{1,0:T(8,128)(2,1)}) %all-gather.5.cloned.1.call-update) | async-done | bytes 2097168 | tf_op jit(solution)/shard_map/all_gather | solution.py:45
  64.3 4.6 fusion.25
  68.9 55.1 %all_to_all.31 = f32[8,128,1024]{2,1,0:T(8,128)} all-to-all(f32[8,128,1024]{2,1,0:T(8,128)S(1)} %fusion.25), channel_id=1, replica_groups=mesh['blk'=16,'seq'=8] {'seq'}, dimensions={0} | all-to-all | bytes 8388608 | tf_op jit(solution)/shard_map/all_to_all | solution.py:18
  124.0 3.4 reduce_sum.66
  127.5 0.0 all-gather.7.cloned.1.call-update
  127.5 0.0 all-gather.9.cloned.1.call-start
  127.6 1.2 copy.90
  128.8 2.3 copy.59
  131.0 17.0 %all-gather = s32[1,1024]{1,0:T(1,128)S(1)} all-gather(s32[1,128]{1,0:T(1,128)S(1)} %copy-done.6), channel_id=2, replica_groups=mesh['blk'=16,'seq'=8] {'seq'}, dimensions={1}, use_global_device_ids=true | all-gather | bytes 4608 | tf_op jit(solution)/shard_map/all_gather | solution.py:70
  148.1 0.2 fusion.32
  148.3 30.3 %all-gather.7.cloned.1.call-done = bf16[1024,1024]{1,0:T(8,128)(2,1)} async-done(((bf16[128,1024]{1,0:T(8,128)(2,1)}), bf16[1024,1024]{1,0:T(8,128)(2,1)}) %all-gather.7.cloned.1.call-update) | async-done | bytes 2097168 | tf_op jit(solution)/shard_map/all_gather | solution.py:69
  178.5 3.0 fusion.36
  181.5 1.5 copy.54
  183.0 9.1 %fusion.37 = (f32[4,8,128]{2,1,0:T(8,128)S(1)}, f32[4,8,128,1024]{2,3,1,0:T(8,128)}) fusion(bf16[1024,4,128,1]{0,2,3,1:T(8,128)(2,1)S(1)} %bitcast.121, bf16[128,4,8,128]{3,2,1,0:T(8,128)(2,1)} %bitcast.123, pred[128,1024]{0,1:T(8,128)(4,1)S(1)} %fusion.32), kind=kOutput, calls=%fused_computation.63 | convolution fusion | flops 1086320640 | bytes 19021824 | tf_op jit(solution)/shard_map/qgjd,kgd->gjqk/dot_general | solution.py:55
  192.1 2.3 copy.57
  194.4 8.7 %fusion.1 = f32[4,8,128]{2,1,0:T(8,128)S(1)} fusion(f32[4,8,128,1024]{2,3,1,0:T(8,128)} %get-tuple-element.33, f32[4,8,128]{2,1,0:T(8,128)S(1)} %broadcast_maximum_fusion, pred[128,1024]{0,1:T(8,128)(4,1)S(1)} %fusion.32), kind=kLoop, calls=%fused_computation.5 | loop fusion | flops 12578816 | bytes 16941056 | tf_op jit(solution)/shard_map/reduce_sum | solution.py:78
  203.1 9.9 %fusion.24 = (bf16[128,4,8,128]{0,3,2,1:T(8,128)(2,1)}, f32[4,8,128,128]{2,3,1,0:T(8,128)S(1)}) fusion(f32[128,4,8]{0,2,1:T(8,128)S(1)} %bitcast.146, bf16[1024,4,128,1]{0,2,3,1:T(8,128)(2,1)S(1)} %bitcast.144, f32[4,8,128,1024]{2,3,1,0:T(8,128)} %get-tuple-element.33, f32[4,8,128]{2,1,0:T(8,128)S(1)} %broadcast_maximum_fusion, ...), kind=kOutput, calls=%fused_computation.34 | convolution fusion | flops 1087373312 | bytes 21135360 | tf_op jit(solution)/shard_map/gjqk,kgd->gjqd/dot_general | solution.py:77
  212.9 0.5 multiply_reduce_fusion.1
  213.4 9.5 %fusion.27 = f32[1024,4,128]{2,0,1:T(8,128)} fusion(bf16[4,8,128,128]{2,3,1,0:T(8,128)(2,1)S(1)} %bitcast.130, f32[4,8,128,1024]{2,3,1,0:T(8,128)} %get-tuple-element.33, f32[4,8,128]{2,1,0:T(8,128)S(1)} %log_add_fusion, pred[128,1024]{0,1:T(8,128)(4,1)S(1)} %fusion.32), kind=kOutput, calls=%fused_computation.41 | convolution fusion | flops 1086324736 | bytes 20070400 | tf_op jit(solution)/shard_map/gjqk,gjqd->kgd/dot_general | solution.py:96
  222.9 10.3 %fusion = bf16[4,8,128,1024]{2,3,1,0:T(8,128)(2,1)} fusion(f32[4,8,128,1024]{2,3,1,0:T(8,128)} %get-tuple-element.33, bf16[1024,4,128,1]{0,2,3,1:T(8,128)(2,1)S(1)} %bitcast.145, bf16[4,8,128,128]{2,3,1,0:T(8,128)(2,1)S(1)} %bitcast.131, f32[4,8,128]{2,1,0:T(8,128)S(1)} %multiply_reduce_fusion.1, f32[4,8,128]{2,1,0:T(8,128)S(1)} %log_add_fusion, ...), kind=kOutput, calls=%fused_computation.1 | convolution fusion | flops 1094713344 | bytes 27426816 | tf_op jit(solution)/shard_map/gjqd,kgd->gjqk/dot_general | solution.py:93
  233.3 2.9 copy.66
  236.2 3.5 copy.92
  239.7 7.1 %fusion.23 = f32[1024,4,128]{2,0,1:T(8,128)} fusion(bf16[4,8,128,1024]{2,3,1,0:T(8,128)(2,1)} %fusion, bf16[128,4,8,128]{3,2,1,0:T(8,128)(2,1)S(1)} %bitcast.124), kind=kOutput, calls=%fused_computation.32 | convolution fusion | flops 1074266112 | bytes 11534336 | tf_op jit(solution)/shard_map/gjqk,qgjd->kgd/dot_general | solution.py:98
  246.8 2.9 copy.64
  249.6 2.2 copy.91
  251.9 0.3 pad_maximum_fusion
  252.1 0.8 copy.67
  253.0 50.9 %all_to_all.32 = f32[8,128,1024]{1,2,0:T(8,128)} all-to-all(f32[8,128,1024]{1,2,0:T(8,128)S(1)} %copy.67), channel_id=1, replica_groups=mesh['blk'=16,'seq'=8] {'seq'}, dimensions={0} | all-to-all | bytes 8388608 | tf_op jit(solution)/shard_map/all_to_all | solution.py:18
  303.9 3.2 reduce_sum.69
  307.1 0.0 all-gather.9.cloned.1.call-update
  307.1 0.3 reduce-scatter.2.cloned.1.call-start
  307.4 4.7 copy.70
  312.1 51.5 %all-gather.9.cloned.1.call-done = bf16[1024,1024]{0,1:T(8,128)(2,1)} async-done(((bf16[128,1024]{0,1:T(8,128)(2,1)}), bf16[1024,1024]{0,1:T(8,128)(2,1)}) %all-gather.9.cloned.1.call-update) | async-done | bytes 2097168 | tf_op jit(solution)/shard_map/all_gather | solution.py:111
  363.6 6.5 %fusion.20 = f32[1024,1024]{1,0:T(8,128)} fusion(bf16[1024,1024]{0,1:T(8,128)(2,1)} %all-gather.9.cloned.1.call-done, bf16[128,8,8,128]{3,2,1,0:T(8,128)(2,1)} %bitcast.133), kind=kOutput, calls=%fused_computation.28 | convolution fusion | flops 2147483648 | bytes 8388608 | tf_op jit(solution)/shard_map/dot_general | solution.py:115
  370.1 4.5 convolution_convert_fusion
  374.7 0.4 fusion.35
  375.1 0.7 constant_dynamic-update-slice_fusion.7
  375.8 0.7 constant_dynamic-update-slice_fusion.6
  376.5 0.7 constant_dynamic-update-slice_fusion.5
  377.2 0.7 constant_dynamic-update-slice_fusion.4
  378.0 0.7 constant_dynamic-update-slice_fusion.3
  378.7 0.7 constant_dynamic-update-slice_fusion.2
  379.4 0.7 constant_dynamic-update-slice_fusion.1
  380.1 0.7 constant_dynamic-update-slice_fusion
  380.8 4.3 all-to-all-start.3
  385.2 2.3 copy.71
  387.5 5.8 %multiply_convert_fusion.1 = bf16[4,128,8,128]{3,1,2,0:T(8,128)(2,1)} fusion(bf16[1024,4,128,1]{0,2,3,1:T(8,128)(2,1)S(1)} %bitcast.122, bf16[4,8,128,1024]{2,3,1,0:T(8,128)(2,1)} %fusion), kind=kOutput, calls=%fused_computation.37 | convolution fusion | flops 1074790400 | bytes 10485760 | tf_op jit(solution)/shard_map/gjqk,kgd->qgjd/dot_general | solution.py:102
  393.2 2.3 copy.72
  395.5 22.0 %all-to-all-done.3 = bf16[8,128,16,1,64]{1,4,2,3,0:T(8,128)(2,1)} async-done(((bf16[8,128,16,1,64]{1,4,2,3,0:T(8,128)(2,1)}), bf16[8,128,16,1,64]{1,4,2,3,0:T(8,128)(2,1)}, u32[]{:S(2)}, u32[]{:S(2)}) %all-to-all-start.3) | async-done | bytes 2097184 | tf_op jit(solution)/shard_map/all_to_all | solution.py:125
  417.5 4.3 fusion.17
  421.8 3.5 fusion.16
  425.3 4.1 copy.73
  429.4 0.1 reduce_sum.72
  429.4 69.3 %psum.7 = f32[8192]{0:T(1024)} all-reduce(f32[8192]{0:T(1024)S(1)} %reduce_sum.72), channel_id=1, replica_groups=mesh['blk'=16,'seq'=8] {'blk','seq'}, use_global_device_ids=true, to_apply=%region_9.10 | all-reduce | flops 8192 | bytes 65536 | tf_op jit(solution)/shard_map/psum | solution.py:129
  (21 shorter events, 0.1 us)
Async XLA Ops:
  7.2 57.1 %all-gather.5.cloned.1.call-start = ((), (), s32[]{:S(2)}) async-start(), calls=%async_computation.5 | async-start | bytes 2228224 | tf_op jit(solution)/shard_map/all_gather | solution.py:45
  7.9 170.6 %all-gather.7.cloned.1.call-start = ((), (), s32[]{:S(2)}) async-start(), calls=%async_computation.6 | async-start | bytes 2359296 | tf_op jit(solution)/shard_map/all_gather | solution.py:69
  11.2 2.3 copy-start.5
  124.0 3.5 copy-start.3
  127.5 236.1 %all-gather.9.cloned.1.call-start = ((), (), s32[]{:S(2)}) async-start(), calls=%async_computation.7 | async-start | bytes 2359296 | tf_op jit(solution)/shard_map/all_gather | solution.py:111
  127.6 3.5 copy-start.6
  194.4 8.7 %copy-start.4 = (bf16[1024,512]{0,1:T(8,128)(2,1)S(1)}, bf16[1024,512]{0,1:T(8,128)(2,1)}, u32[]{:S(2)}) copy-start(bf16[1024,512]{0,1:T(8,128)(2,1)} %copy.57) | copy-start | bytes 3145732
  203.1 9.9 %copy-start.2 = (bf16[1,128,4096]{1,2,0:T(8,128)(2,1)S(1)}, bf16[1,128,4096]{1,2,0:T(8,128)(2,1)}, u32[]{:S(2)}) copy-start(bf16[1,128,4096]{1,2,0:T(8,128)(2,1)} %copy.59) | copy-start | bytes 3145732
  236.2 3.5 copy-start
  249.6 2.2 copy-start.1
  307.1 191.6 %reduce-scatter.2.cloned.1.call-start = ((), (), s32[]{:S(2)}) async-start(), calls=%async_computation.8 | async-start | bytes 4456448 | tf_op jit(solution)/shard_map/reduce_scatter | solution.py:114
  380.8 36.7 %all-to-all-start.3 = ((bf16[8,128,16,1,64]{1,4,2,3,0:T(8,128)(2,1)}), bf16[8,128,16,1,64]{1,4,2,3,0:T(8,128)(2,1)}, u32[]{:S(2)}, u32[]{:S(2)}) async-start(bf16[8,128,16,1,64]{1,4,2,3,0:T(8,128)(2,1)} %constant_dynamic-update-slice_fusion), calls=%async_computation.3 | async-start | bytes 4194304 | tf_op jit(solution)/shard_map/all_to_all | solution.py:125
Sparse Core Ops, SparseCore 0:
  9.7 54.5 all-gather.4
  127.6 50.8 all-gather.6
  307.2 56.3 all-gather.8
  370.2 71.6 reduce-scatter.1
